TPU v7x, 32 devices: a whole 2x2x4 slice. The times are simulated.
32 devices in a mesh: slab: 2 (over y), date: 8 (over z, x), tile: 1, sub: 2 (over core).
Axes of the slice: x: 2, y: 2, z: 4, core: 2. Of those that a mesh axis runs over, the one named last changes fastest.
Arguments:
- slc: bfloat16 [2, 100, 128, 512], P(None, None, 'date', ('slab', 'tile', 'sub')), parts along dimension 3, may hold values from -300 to 300, as said below
- usable: int32 [100, 128, 512], P(None, 'date', ('slab', 'tile', 'sub')), parts along dimension 2, may hold values 0 or 1
Outputs:
- coherence: bfloat16 [2, 4, 8, 16, 128, 128], P(None, ('slab', 'tile', 'sub'), 'date'), parts along dimension 1
- linked: float32 [2, 128, 512], P(None, 'date', ('slab', 'tile', 'sub')), parts along dimension 2
There are 2 independent parts, one for each index of `slab`. A program takes and returns all parts, laid end to end along the dimension named above; each array names one. Nothing has to cross between parts.
Inputs may be any that keep to these rules, and one draw needn't show every extreme that they name: `slc`: complex samples of a partly coherent stack.
All inputs are finite; a program needn't handle non-finite values. No bound on the sum of `usable` on one device may be relied on, other than what follows from the above.
Results may differ from a plain program's by a relative error of at most 0.0016.
Values may be sent and summed in bfloat16 or wider, within the bound.
A program may use at most 64 MiB of HBM per device.

v0:
```python
import jax
import jax.numpy as jnp
from jax import lax
from jax.sharding import PartitionSpec as P

ITERS = 4


def inverse_roots(block):
    samples = block.astype(jnp.float32)
    intensity = jnp.mean(samples[0] * samples[0] + samples[1] * samples[1], axis=0) + 1e-05
    return lax.rsqrt(intensity)


def pair_terms(left_block, right_block, left_root, right_root, looks_count):
    real_sum = jnp.einsum(
        "law,lbw->wab", left_block[0], right_block[0], preferred_element_type=jnp.float32
    )
    real_sum = real_sum + jnp.einsum(
        "law,lbw->wab", left_block[1], right_block[1], preferred_element_type=jnp.float32
    )
    imag_sum = jnp.einsum(
        "law,lbw->wab", left_block[1], right_block[0], preferred_element_type=jnp.float32
    )
    imag_sum = imag_sum - jnp.einsum(
        "law,lbw->wab", left_block[0], right_block[1], preferred_element_type=jnp.float32
    )
    factor = left_root.T[:, :, None] * right_root.T[:, None, :] * (1.0 / looks_count)
    return jnp.stack([real_sum * factor, imag_sum * factor])


def local_pairs(samples, looks_count):
    window_root = inverse_roots(samples)
    return pair_terms(samples, samples, window_root, window_root, looks_count).astype(jnp.bfloat16)


def complex_apply(matrix, vec_real, vec_imag):
    rr = jnp.einsum("wab,bw->aw", matrix[0], vec_real, precision=lax.Precision.HIGHEST)
    ii = jnp.einsum("wab,bw->aw", matrix[1], vec_imag, precision=lax.Precision.HIGHEST)
    ri = jnp.einsum("wab,bw->aw", matrix[0], vec_imag, precision=lax.Precision.HIGHEST)
    ir = jnp.einsum("wab,bw->aw", matrix[1], vec_real, precision=lax.Precision.HIGHEST)
    return (rr - ii, ri + ir)


def local(slc, usable):
    masked = slc * usable.astype(jnp.bfloat16)[None]
    looks_count = slc.shape[1]
    own_dates = slc.shape[2]
    windows = slc.shape[3]
    blocks_count = lax.axis_size("date")
    all_dates = own_dates * blocks_count
    per_device = windows // blocks_count
    split_view = masked.reshape(2, looks_count, own_dates, blocks_count, per_device)
    result = local_pairs(
        lax.all_to_all(split_view, "date", split_axis=3, concat_axis=2, tiled=True)[:, :, :, 0, :],
        looks_count,
    )
    matrix = result.astype(jnp.float32)
    vec_real = jnp.ones((all_dates, per_device), jnp.float32)
    vec_imag = jnp.zeros((all_dates, per_device), jnp.float32)
    for step in range(ITERS):
        new_real, new_imag = complex_apply(matrix, vec_real, vec_imag)
        scale = lax.rsqrt(jnp.mean(new_real * new_real + new_imag * new_imag, axis=0) + 1e-05)
        vec_real = new_real * scale[None]
        vec_imag = new_imag * scale[None]
    linked = lax.all_to_all(
        jnp.stack([vec_real, vec_imag]), "date", split_axis=1, concat_axis=2, tiled=True
    )
    return (result.reshape(2, 1, 1, per_device, all_dates, all_dates), linked)


def solution(mesh):
    return jax.shard_map(
        local,
        mesh=mesh,
        in_specs=(
            P(None, None, "date", ("slab", "tile", "sub")),
            P(None, "date", ("slab", "tile", "sub")),
        ),
        out_specs=(
            P(None, ("slab", "tile", "sub"), "date", None, None, None),
            P(None, "date", ("slab", "tile", "sub")),
        ),
        check_vma=False,
    )
```

profile of v0, /device:TPU:0, one launch (start us, length us, event | category | flops | bytes accessed | tf_op | source)
XLA Modules:
  0.0 69.2 jit_solution(11306917477091956717)
XLA Ops:
  0.6 1.9 %copy.78 = bf16[2,100,16,128]{1,3,2,0:T(8,128)(2,1)S(1)} copy(bf16[2,100,16,128]{3,2,1,0:T(8,128)(2,1)} %param.2) | data formatting | bytes 1638400 | tf_op args[0]
  2.7 0.4 copy.77
  3.5 32.8 %all_to_all.33 = bf16[2,100,16,8,16]{1,4,2,0,3:T(8,128)(2,1)S(1)} all-to-all(bf16[2,100,16,8,16]{1,4,2,0,3:T(8,128)(2,1)S(1)} %copy.79), channel_id=1, replica_groups=mesh['slab'=2,'date'=8,'tile'=1,'sub'=2] {'date'}, dimensions={3} | all-to-all | bytes 1638400 | tf_op jit(solution)/shard_map/all_to_all | solution.py:55
  36.6 0.5 copy.80
  37.1 0.5 copy.82
  37.9 0.4 fusion.5
  38.8 0.5 fusion.3
  39.3 0.9 %fusion.10 = f32[16,1,128]{2,1,0:T(1,128)S(1)} fusion(bf16[16,128,128]{2,1,0:T(8,128)(2,1)S(1)} %fusion.3), kind=kOutput, calls=%fused_computation.26 | convolution fusion | flops 3145728 | bytes 532480 | tf_op jit(solution)/shard_map/wab,bw->aw/dot_general | solution.py:39
  40.3 0.9 %fusion.12 = f32[16,1,128]{2,1,0:T(1,128)S(1)} fusion(bf16[16,128,128]{2,1,0:T(8,128)(2,1)S(1)} %fusion.3), kind=kOutput, calls=%fused_computation.28 | convolution fusion | flops 3145728 | bytes 532480 | tf_op jit(solution)/shard_map/wab,bw->aw/dot_general | solution.py:41
  41.2 0.4 fusion.21
  41.6 0.5 fusion.2
  42.1 0.9 %fusion.14 = f32[16,1,128]{2,1,0:T(1,128)S(1)} fusion(bf16[16,128,128]{2,1,0:T(8,128)(2,1)S(1)} %fusion.2), kind=kOutput, calls=%fused_computation.30 | convolution fusion | flops 3145728 | bytes 532480 | tf_op jit(solution)/shard_map/wab,bw->aw/dot_general | solution.py:38
  43.0 0.9 %fusion.8 = f32[16,1,128]{2,1,0:T(1,128)S(1)} fusion(bf16[16,128,128]{2,1,0:T(8,128)(2,1)S(1)} %fusion.2), kind=kOutput, calls=%fused_computation.24 | convolution fusion | flops 3145728 | bytes 532480 | tf_op jit(solution)/shard_map/wab,bw->aw/dot_general | solution.py:40
  44.1 0.9 %fusion.25 = f32[16,1,128]{2,1,0:T(1,128)S(1)} fusion(f32[128,16,1]{0,2,1:T(1,128)S(1)} %bitcast.144, bf16[16,128,128]{2,1,0:T(8,128)(2,1)S(1)} %fusion.2), kind=kOutput, calls=%fused_computation.52 | convolution fusion | flops 3145728 | bytes 540672 | tf_op jit(solution)/shard_map/wab,bw->aw/dot_general | solution.py:40
  45.1 0.9 %fusion.24 = f32[16,1,128]{2,1,0:T(1,128)S(1)} fusion(f32[128,16,1]{0,2,1:T(1,128)S(1)} %bitcast.145, bf16[16,128,128]{2,1,0:T(8,128)(2,1)S(1)} %fusion.3), kind=kOutput, calls=%fused_computation.51 | convolution fusion | flops 3145728 | bytes 540672 | tf_op jit(solution)/shard_map/wab,bw->aw/dot_general | solution.py:39
  46.0 0.9 %fusion.26 = f32[16,1,128]{2,1,0:T(1,128)S(1)} fusion(f32[128,16,1]{0,2,1:T(1,128)S(1)} %bitcast.138, bf16[16,128,128]{2,1,0:T(8,128)(2,1)S(1)} %fusion.3), kind=kOutput, calls=%fused_computation.53 | convolution fusion | flops 3145728 | bytes 540672 | tf_op jit(solution)/shard_map/wab,bw->aw/dot_general | solution.py:41
  46.9 0.9 %fusion.23 = f32[16,1,128]{2,1,0:T(1,128)S(1)} fusion(f32[128,16,1]{0,2,1:T(1,128)S(1)} %bitcast.139, bf16[16,128,128]{2,1,0:T(8,128)(2,1)S(1)} %fusion.2), kind=kOutput, calls=%fused_computation.50 | convolution fusion | flops 3145728 | bytes 540672 | tf_op jit(solution)/shard_map/wab,bw->aw/dot_general | solution.py:38
  48.0 0.9 %fusion.29 = f32[16,1,128]{2,1,0:T(1,128)S(1)} fusion(f32[128,16,1]{0,2,1:T(1,128)S(1)} %bitcast.146, bf16[16,128,128]{2,1,0:T(8,128)(2,1)S(1)} %fusion.2), kind=kOutput, calls=%fused_computation.56 | convolution fusion | flops 3145728 | bytes 540672 | tf_op jit(solution)/shard_map/wab,bw->aw/dot_general | solution.py:40
  49.0 0.9 %fusion.28 = f32[16,1,128]{2,1,0:T(1,128)S(1)} fusion(f32[128,16,1]{0,2,1:T(1,128)S(1)} %bitcast.147, bf16[16,128,128]{2,1,0:T(8,128)(2,1)S(1)} %fusion.3), kind=kOutput, calls=%fused_computation.55 | convolution fusion | flops 3145728 | bytes 540672 | tf_op jit(solution)/shard_map/wab,bw->aw/dot_general | solution.py:39
  49.9 0.9 %fusion.30 = f32[16,1,128]{2,1,0:T(1,128)S(1)} fusion(f32[128,16,1]{0,2,1:T(1,128)S(1)} %bitcast.140, bf16[16,128,128]{2,1,0:T(8,128)(2,1)S(1)} %fusion.3), kind=kOutput, calls=%fused_computation.57 | convolution fusion | flops 3145728 | bytes 540672 | tf_op jit(solution)/shard_map/wab,bw->aw/dot_general | solution.py:41
  50.8 0.9 %fusion.27 = f32[16,1,128]{2,1,0:T(1,128)S(1)} fusion(f32[128,16,1]{0,2,1:T(1,128)S(1)} %bitcast.141, bf16[16,128,128]{2,1,0:T(8,128)(2,1)S(1)} %fusion.2), kind=kOutput, calls=%fused_computation.54 | convolution fusion | flops 3145728 | bytes 540672 | tf_op jit(solution)/shard_map/wab,bw->aw/dot_general | solution.py:38
  52.0 0.9 %fusion.33 = f32[16,1,128]{2,1,0:T(1,128)S(1)} fusion(f32[128,16,1]{0,2,1:T(1,128)S(1)} %bitcast.148, bf16[16,128,128]{2,1,0:T(8,128)(2,1)S(1)} %fusion.2), kind=kOutput, calls=%fused_computation.60 | convolution fusion | flops 3145728 | bytes 540672 | tf_op jit(solution)/shard_map/wab,bw->aw/dot_general | solution.py:40
  52.9 0.9 %fusion.32 = f32[16,1,128]{2,1,0:T(1,128)S(1)} fusion(f32[128,16,1]{0,2,1:T(1,128)S(1)} %bitcast.149, bf16[16,128,128]{2,1,0:T(8,128)(2,1)S(1)} %fusion.3), kind=kOutput, calls=%fused_computation.59 | convolution fusion | flops 3145728 | bytes 540672 | tf_op jit(solution)/shard_map/wab,bw->aw/dot_general | solution.py:39
  53.8 0.9 %fusion.34 = f32[16,1,128]{2,1,0:T(1,128)S(1)} fusion(f32[128,16,1]{0,2,1:T(1,128)S(1)} %bitcast.142, bf16[16,128,128]{2,1,0:T(8,128)(2,1)S(1)} %fusion.3), kind=kOutput, calls=%fused_computation.61 | convolution fusion | flops 3145728 | bytes 540672 | tf_op jit(solution)/shard_map/wab,bw->aw/dot_general | solution.py:41
  54.7 0.9 %fusion.31 = f32[16,1,128]{2,1,0:T(1,128)S(1)} fusion(f32[128,16,1]{0,2,1:T(1,128)S(1)} %bitcast.143, bf16[16,128,128]{2,1,0:T(8,128)(2,1)S(1)} %fusion.2), kind=kOutput, calls=%fused_computation.58 | convolution fusion | flops 3145728 | bytes 540672 | tf_op jit(solution)/shard_map/wab,bw->aw/dot_general | solution.py:38
  56.0 0.8 %reshape.118 = f32[8,1,512]{2,1,0:T(1,128)} reshape(f32[128,2,16]{2,1,0:T(2,128)S(1)} %bitcast.133) | data formatting | bytes 32768
  56.8 3.6 %all-to-all-start.1 = ((f32[8,1,512]{2,1,0:T(1,128)}), f32[8,1,512]{2,1,0:T(1,128)S(1)}, u32[]{:S(2)}, u32[]{:S(2)}) async-start(f32[8,1,512]{2,1,0:T(1,128)} %reshape.118), calls=%async_computation.1 | async-start | bytes 32768 | tf_op jit(solution)/shard_map/all_to_all | solution.py:66
  60.4 1.1 %pad_maximum_fusion = bf16[2,1,1,16,128,128]{5,4,3,2,1,0:T(8,128)(2,1)} fusion(bf16[1,1,1,16,128,128]{5,4,3,2,1,0:T(8,128)(2,1)S(1)} %bitcast.127, bf16[1,1,1,16,128,128]{5,4,3,2,1,0:T(8,128)(2,1)S(1)} %bitcast.128), kind=kLoop, calls=%fused_computation.10 | loop fusion | flops 524288 | bytes 2097152 | tf_op jit(solution)/shard_map/stack | solution.py:29
  61.5 5.5 %all-to-all-done.1 = f32[8,1,512]{2,1,0:T(1,128)S(1)} async-done(((f32[8,1,512]{2,1,0:T(1,128)}), f32[8,1,512]{2,1,0:T(1,128)S(1)}, u32[]{:S(2)}, u32[]{:S(2)}) %all-to-all-start.1) | async-done | bytes 16416 | tf_op jit(solution)/shard_map/all_to_all | solution.py:66
  67.0 0.5 broadcast.84
  67.5 0.7 reduce.7
  68.5 0.7 %all_to_all.30 = f32[2,16,128]{2,1,0:T(8,128)} reshape(f32[2,16,8,16]{3,2,1,0:T(8,128)S(1)} %bitcast.135) | data formatting | bytes 32768 | tf_op jit(solution)/shard_map/all_to_all | solution.py:66
  (27 shorter events, 2.7 us)
Async XLA Ops:
  0.6 2.0 %copy-start = (s32[100,16,128]{2,1,0:T(8,128)S(1)}, s32[100,16,128]{2,1,0:T(8,128)}, u32[]{:S(2)}) copy-start(s32[100,16,128]{2,1,0:T(8,128)} %param.3) | copy-start | bytes 2457604
  56.8 10.2 %all-to-all-start.1 = ((f32[8,1,512]{2,1,0:T(1,128)}), f32[8,1,512]{2,1,0:T(1,128)S(1)}, u32[]{:S(2)}, u32[]{:S(2)}) async-start(f32[8,1,512]{2,1,0:T(1,128)} %reshape.118), calls=%async_computation.1 | async-start | bytes 32768 | tf_op jit(solution)/shard_map/all_to_all | solution.py:66
where the time goes:
time: 69.4 us; the launch traced here: 69.2 us
  blocking collectives  32.8 us (47%)
  matrix products  16.5 us (24%)
  local copies, waits for them, and re-layouts  6.56 us (9%)
  waiting for transfers between devices  5.51 us (8%)
  starting transfers between devices  3.59 us (5%)
  other arithmetic  3.35 us (5%)
  between operations  0.82 us (1%)
    all_to_all x1, blocking collectives, local(): lax.all_to_all(split_view, 'date', split_axis=3, concat_axis=2, tiled=True)  32.8 us
    all_to_all x1, waiting for transfers between devices, local(): lax.all_to_all(jnp.stack([vec_real, vec_imag]), 'date', split_axis=1, con...  5.51 us
    dot_general x4, matrix products, complex_apply(): jnp.einsum('wab,bw->aw', matrix[1], vec_real, precision=lax.Precision.HIG...  3.7 us
    dot_general x4, matrix products, complex_apply(): jnp.einsum('wab,bw->aw', matrix[0], vec_imag, precision=lax.Precision.HIG...  3.68 us
    dot_general x4, matrix products, complex_apply(): jnp.einsum('wab,bw->aw', matrix[0], vec_real, precision=lax.Precision.HIG...  3.68 us
    dot_general x4, matrix products, complex_apply(): jnp.einsum('wab,bw->aw', matrix[1], vec_imag, precision=lax.Precision.HIG...  3.68 us
    all_to_all x1, starting transfers between devices, local(): lax.all_to_all(jnp.stack([vec_real, vec_imag]), 'date', split_axis=1, con...  3.59 us
    unnamed x5, local copies, waits for them, and re-layouts  2.95 us
  transfers between devices with their start and end apart: 1, of which 1 were waited for; matrix products, arithmetic and copies ran while one was open for 2% of the time, Pallas kernels for 0%

commit v1 on v0

v1 whole, which is shorter than its diff:
```python
import functools

import jax
import jax.numpy as jnp
from jax import lax
from jax.experimental import pallas as pl
from jax.experimental.pallas import tpu as pltpu
from jax.sharding import PartitionSpec as P

ITERS = 4
LANES = 128
NT = (((1,), (1,)), ((), ()))


def dot_nt(left, right):
    return lax.dot_general(left, right, NT, preferred_element_type=jnp.float32)


def window_coherence(real, imag, looks_count):
    dates = real.shape[0]
    plain = jnp.concatenate([real, imag], axis=1)
    swapped = jnp.concatenate([imag, -real], axis=1)
    sums = dot_nt(jnp.concatenate([plain, swapped], axis=0), plain)
    real_sum, imag_sum = sums[:dates], sums[dates:]
    rows = lax.broadcasted_iota(jnp.int32, (dates, dates), 0)
    columns = lax.broadcasted_iota(jnp.int32, (dates, dates), 1)
    diagonal = jnp.where(rows == columns, real_sum, 0.0)
    row_root = lax.rsqrt(jnp.sum(diagonal, axis=0, keepdims=True) * (1.0 / looks_count) + 1e-05)
    column_root = lax.rsqrt(jnp.sum(diagonal, axis=1, keepdims=True) * (1.0 / looks_count) + 1e-05)
    factor = column_root * row_root * (1.0 / looks_count)
    return (real_sum * factor).astype(jnp.bfloat16), (imag_sum * factor).astype(jnp.bfloat16)


def link_windows(matrices):
    dates = matrices[0].shape[1]
    row = lax.broadcasted_iota(jnp.int32, (8, dates), 0)
    is_real = row < 3
    is_imag = jnp.logical_and(row >= 3, row < 6)
    is_first = jnp.logical_or(row == 0, row == 3)
    is_second = jnp.logical_or(row == 1, row == 4)
    state = [jnp.where(is_real, 1.0, 0.0)] * len(matrices)
    result = None
    for step in range(ITERS):
        products = []
        for vec, matrix in zip(state, matrices):
            high = vec.astype(jnp.bfloat16).astype(jnp.float32)
            rest = vec - high
            middle = rest.astype(jnp.bfloat16).astype(jnp.float32)
            parts = jnp.where(is_first, high, jnp.where(is_second, middle, rest - middle))
            products.append(dot_nt(parts.astype(jnp.bfloat16), matrix))
        state, result = [], []
        for product in products:
            first, second = product[:, :dates], product[:, dates:]
            zero = jnp.zeros_like(first)
            new_real = jnp.sum(
                jnp.where(is_real, first, jnp.where(is_imag, -second, zero)), axis=0, keepdims=True
            )
            new_imag = jnp.sum(
                jnp.where(is_real, second, jnp.where(is_imag, first, zero)), axis=0, keepdims=True
            )
            power = jnp.sum(new_real * new_real + new_imag * new_imag, axis=1, keepdims=True)
            scale = lax.rsqrt(power * (1.0 / dates) + 1e-05)
            new_real = new_real * scale
            new_imag = new_imag * scale
            result.append((new_real, new_imag))
            state.append(
                jnp.where(
                    is_real,
                    jnp.broadcast_to(new_real, (8, dates)),
                    jnp.where(is_imag, jnp.broadcast_to(new_imag, (8, dates)), 0.0),
                )
            )
    return result


def kernel(
    count, looks_count, group,
    send_ref, coherence_ref, linked_ref,
    held, matrix, vectors, turned, landed,
    send_sem, recv_sem, own_sem, out_sem, back_send, back_recv,
):
    me = lax.axis_index("date")
    windows = held.shape[0]
    dates = held.shape[2]
    own = dates // count
    groups = windows // group

    barrier = pltpu.get_barrier_semaphore()
    for offset in range(1, count):
        pl.semaphore_signal(
            barrier, inc=1, device_id={"date": lax.rem(me + offset, count)},
            device_id_type=pl.DeviceIdType.MESH,
        )
    pl.semaphore_wait(barrier, count - 1)

    mine = pl.ds(pl.multiple_of(me * own, own), own)

    def block_copy(part, offset):
        span = pl.ds(part * group, group)
        other = lax.rem(me + offset, count)
        return pltpu.make_async_remote_copy(
            src_ref=send_ref.at[other, span],
            dst_ref=held.at[span, :, mine],
            send_sem=send_sem.at[part, offset],
            recv_sem=recv_sem.at[part, offset],
            device_id={"date": other},
            device_id_type=pl.DeviceIdType.MESH,
        )

    own_copy = pltpu.make_async_copy(send_ref.at[me], held.at[:, :, mine], own_sem)
    own_copy.start()

    def start_part(part, carry):
        for offset in range(1, count):
            block_copy(part, offset).start()
        return carry

    lax.fori_loop(0, groups, start_part, 0)
    own_copy.wait()

    def out_copy(part):
        span = pl.ds(part * group, group)
        return pltpu.make_async_copy(
            matrix.at[:, span], coherence_ref.at[:, 0, 0, span], out_sem.at[part]
        )

    def compute_part(part, carry):
        for offset in range(1, count):
            block_copy(part, offset).wait_recv()
        matrices = []
        for inner in range(group):
            window = part * group + inner
            real, imag = window_coherence(held[window, 0], held[window, 1], looks_count)
            matrix[0, window] = real
            matrix[1, window] = imag
            matrices.append(jnp.concatenate([real, imag], axis=0))
        for inner, (real, imag) in enumerate(link_windows(matrices)):
            vectors[0, pl.ds(part * group + inner, 1)] = real
            vectors[1, pl.ds(part * group + inner, 1)] = imag
        out_copy(part).start()
        return carry

    lax.fori_loop(0, groups, compute_part, 0)

    turned[:, : 2 * windows] = jnp.concatenate([vectors[0], vectors[1]], axis=0).T

    def back_copy(offset):
        other = lax.rem(me + offset, count)
        return pltpu.make_async_remote_copy(
            src_ref=turned.at[pl.ds(pl.multiple_of(other * own, own), own)],
            dst_ref=landed.at[me],
            send_sem=back_send.at[offset],
            recv_sem=back_recv.at[offset],
            device_id={"date": other},
            device_id_type=pl.DeviceIdType.MESH,
        )

    for offset in range(1, count):
        back_copy(offset).start()
    landed[me] = turned[mine]
    for offset in range(1, count):
        back_copy(offset).wait_recv()
    for side in range(2):
        linked_ref[side] = jnp.concatenate(
            [landed[source][:, side * windows : (side + 1) * windows] for source in range(count)], axis=1
        )

    def finish_part(part, carry):
        for offset in range(1, count):
            block_copy(part, offset).wait_send()
        out_copy(part).wait()
        return carry

    lax.fori_loop(0, groups, finish_part, 0)
    for offset in range(1, count):
        back_copy(offset).wait_send()


def local(slc, usable):
    looks_count, own_dates, windows = usable.shape
    count = lax.axis_size("date")
    per_device = windows // count
    dates = own_dates * count
    masked = slc * usable.astype(jnp.bfloat16)[None]
    padded_looks = pl.cdiv(looks_count, LANES) * LANES
    blocks = jnp.transpose(
        masked.reshape(2, looks_count, own_dates, count, per_device), (3, 4, 0, 2, 1)
    )
    blocks = jnp.pad(blocks, ((0, 0),) * 4 + ((0, padded_looks - looks_count),))
    group = next(size for size in (4, 2, 1) if per_device % size == 0)
    groups = per_device // group
    return pl.pallas_call(
        functools.partial(kernel, count, looks_count, group),
        out_shape=(
            jax.ShapeDtypeStruct((2, 1, 1, per_device, dates, dates), jnp.bfloat16),
            jax.ShapeDtypeStruct((2, own_dates, windows), jnp.float32),
        ),
        in_specs=[pl.BlockSpec(memory_space=pltpu.VMEM)],
        out_specs=(
            pl.BlockSpec(memory_space=pl.ANY),
            pl.BlockSpec(memory_space=pltpu.VMEM),
        ),
        scratch_shapes=[
            pltpu.VMEM((per_device, 2, dates, padded_looks), jnp.bfloat16),
            pltpu.VMEM((2, per_device, dates, dates), jnp.bfloat16),
            pltpu.VMEM((2, per_device, dates), jnp.float32),
            pltpu.VMEM((dates, LANES), jnp.float32),
            pltpu.VMEM((count, own_dates, LANES), jnp.float32),
            pltpu.SemaphoreType.DMA((groups, count)),
            pltpu.SemaphoreType.DMA((groups, count)),
            pltpu.SemaphoreType.DMA,
            pltpu.SemaphoreType.DMA((groups,)),
            pltpu.SemaphoreType.DMA((count,)),
            pltpu.SemaphoreType.DMA((count,)),
        ],
        compiler_params=pltpu.CompilerParams(collective_id=0, has_side_effects=True),
    )(blocks)


def solution(mesh):
    return jax.shard_map(
        local,
        mesh=mesh,
        in_specs=(
            P(None, None, "date", ("slab", "tile", "sub")),
            P(None, "date", ("slab", "tile", "sub")),
        ),
        out_specs=(
            P(None, ("slab", "tile", "sub"), "date", None, None, None),
            P(None, "date", ("slab", "tile", "sub")),
        ),
        check_vma=False,
    )
```

time: 69.4 us -> 46.4 us (0.67)
  Pallas kernels: 0 us -> 38.5 us
  blocking collectives: 32.8 us -> 0 us
  matrix products: 16.5 us -> 0 us
  waiting for transfers between devices: 5.51 us -> 0 us
  starting transfers between devices: 3.59 us -> 0 us
  other arithmetic: 3.35 us -> 1.36 us
  local copies, waits for them, and re-layouts: 6.56 us -> 5.64 us
    pallas_call x0 -> x1, Pallas kernels: none -> 38.5 us  [local(): pl.pallas_call(functools.partial(kernel, count, looks_count, group), out_...]
    all_to_all x1 -> x0, blocking collectives: 32.8 us -> none  [local(): lax.all_to_all(split_view, 'date', split_axis=3, concat_axis=2, tiled=True)]
    dot_general x20 -> x0, matrix products: 16.5 us -> none  [the longest x4 3.7 us: complex_apply(): jnp.einsum('wab,bw->aw', matrix[1], vec_real, precision=lax.Precision.HIG...]
    all_to_all x1 -> x0, waiting for transfers between devices: 5.51 us -> none  [local(): lax.all_to_all(jnp.stack([vec_real, vec_imag]), 'date', split_axis=1, con...]
    all_to_all x1 -> x0, starting transfers between devices: 3.59 us -> none  [local(): lax.all_to_all(jnp.stack([vec_real, vec_imag]), 'date', split_axis=1, con...]
    mul x0 -> x1, local copies, waits for them, and re-layouts: none -> 1.42 us  [local(): masked = slc * usable.astype(jnp.bfloat16)[None]]
    all_to_all x3 -> x0, local copies, waits for them, and re-layouts: 1.3 us -> none  [local(): lax.all_to_all(jnp.stack([vec_real, vec_imag]), 'date', split_axis=1, con...]
    convert_element_type x1, other arithmetic: 0.06 us -> 1.28 us  [local(): masked = slc * usable.astype(jnp.bfloat16)[None]]
  transfers between devices with their start and end apart: 1 -> 0, of which waited for: 1 -> 0; matrix products, arithmetic and copies ran while one was open for 2% -> 0% of each run, Pallas kernels for 0% -> 0%
where the time goes in v1:
time: 46.4 us; the launch traced here: 46.2 us
  Pallas kernels  38.5 us (83%)
  local copies, waits for them, and re-layouts  5.64 us (12%)
  other arithmetic  1.36 us (3%)
  between operations  0.67 us (1%)
    pallas_call x1, Pallas kernels, local(): pl.pallas_call(functools.partial(kernel, count, looks_count, group), out_...  38.5 us
    unnamed x6, local copies, waits for them, and re-layouts  3.03 us
    mul x1, local copies, waits for them, and re-layouts, local(): masked = slc * usable.astype(jnp.bfloat16)[None]  1.42 us
    convert_element_type x1, other arithmetic, local(): masked = slc * usable.astype(jnp.bfloat16)[None]  1.28 us
    pad x1, local copies, waits for them, and re-layouts, local(): blocks = jnp.pad(blocks, ((0, 0),) * 4 + ((0, padded_looks - looks_count),))  1.2 us

profile of v1, /device:TPU:0, one launch (start us, length us, event | category | flops | bytes accessed | tf_op | source)
XLA Modules:
  0.0 46.2 jit_solution(5472773924103697323)
XLA Ops:
  0.6 0.0 copy-start
  0.6 1.3 %convert_element_type.5 = bf16[100,16,128]{2,1,0:T(8,128)(2,1)S(1)} convert(s32[100,16,128]{2,1,0:T(8,128)} %param.3) | non-fusion elementwise | flops 204800 | bytes 1228800 | tf_op jit(solution)/shard_map/convert_element_type | solution.py:184
  1.9 0.1 copy-done
  2.0 0.1 broadcast_multiply_fusion
  2.1 1.4 %copy.4 = bf16[2,100,16,128]{1,2,0,3:T(8,128)(2,1)S(1)} copy(bf16[2,100,16,128]{3,2,1,0:T(8,128)(2,1)S(1)} %broadcast_multiply_fusion) | data formatting | bytes 1638400 | tf_op jit(solution)/shard_map/mul | solution.py:184
  3.5 1.2 %pad.4.send_ref = bf16[8,16,2,16,128]{4,3,2,1,0:T(8,128)(2,1)} pad(bf16[8,16,2,16,100]{4,3,2,1,0:T(8,128)(2,1)S(1)} %bitcast.3, bf16[]{:T(256)} %constant.2.clone.1), padding=0_0x0_0x0_0x0_0x0_28 | pad | bytes 1867778 | tf_op jit(solution)/shard_map/jit(_pad)/pad | solution.py:189
  4.7 38.5 %shard_map.41 = (bf16[2,1,1,16,128,128]{5,4,3,2,1,0:T(8,128)(2,1)}, f32[2,16,128]{2,1,0:T(8,128)}) custom-call(bf16[8,16,2,16,128]{4,3,2,1,0:T(8,128)(2,1)} %pad.4.send_ref), custom_call_target="tpu_custom_call" | custom-call | tf_op jit(solution)/shard_map/pallas_call | solution.py:192
  43.2 0.0 copy-start.1
  43.2 2.3 %copy.7 = bf16[2,1,1,16,128,128]{5,4,3,2,1,0:T(8,128)(2,1)} copy(bf16[2,1,1,16,128,128]{5,4,3,2,1,0:T(8,128)(2,1)} %get-tuple-element.4) | data formatting | bytes 2097152
  45.6 0.0 copy-done.1
  45.6 0.6 %copy.8 = f32[2,16,128]{2,1,0:T(8,128)} copy(f32[2,16,128]{2,1,0:T(8,128)S(1)} %copy-done.1) | data formatting | bytes 32768
Async XLA Ops:
  0.6 1.4 %copy-start = (bf16[2,100,16,128]{3,2,1,0:T(8,128)(2,1)S(1)}, bf16[2,100,16,128]{3,2,1,0:T(8,128)(2,1)}, u32[]{:S(2)}) copy-start(bf16[2,100,16,128]{3,2,1,0:T(8,128)(2,1)} %param.2) | copy-start | bytes 2457604
  43.2 2.3 %copy-start.1 = (f32[2,16,128]{2,1,0:T(8,128)S(1)}, f32[2,16,128]{2,1,0:T(8,128)}, u32[]{:S(2)}) copy-start(f32[2,16,128]{2,1,0:T(8,128)} %get-tuple-element.5) | copy-start | bytes 49156

commit v2 on v1

--- a/solution.py
+++ b/solution.py
@@ -73,11 +73,16 @@
     return result
 
 
+def send_order(count):
+    middle = count // 2
+    return sorted(range(1, count), key=lambda offset: abs(offset - middle))
+
+
 def kernel(
     count, looks_count, group,
-    send_ref, coherence_ref, linked_ref,
-    held, matrix, vectors, turned, landed,
-    send_sem, recv_sem, own_sem, out_sem, back_send, back_recv,
+    block_ref, coherence_ref, linked_ref,
+    packed, arrived, held, matrix, vectors, turned, landed,
+    send_sem, recv_sem, out_sem, back_send, back_recv,
 ):
     me = lax.axis_index("date")
     windows = held.shape[0]
@@ -91,32 +96,38 @@
             barrier, inc=1, device_id={"date": lax.rem(me + offset, count)},
             device_id_type=pl.DeviceIdType.MESH,
         )
-    pl.semaphore_wait(barrier, count - 1)
 
     mine = pl.ds(pl.multiple_of(me * own, own), own)
+    order = send_order(count)
 
     def block_copy(part, offset):
-        span = pl.ds(part * group, group)
         other = lax.rem(me + offset, count)
         return pltpu.make_async_remote_copy(
-            src_ref=send_ref.at[other, span],
-            dst_ref=held.at[span, :, mine],
+            src_ref=packed.at[other, part],
+            dst_ref=arrived.at[part, me],
             send_sem=send_sem.at[part, offset],
             recv_sem=recv_sem.at[part, offset],
             device_id={"date": other},
             device_id_type=pl.DeviceIdType.MESH,
         )
 
-    own_copy = pltpu.make_async_copy(send_ref.at[me], held.at[:, :, mine], own_sem)
-    own_copy.start()
-
-    def start_part(part, carry):
-        for offset in range(1, count):
+    def pack(part, offset):
+        other = lax.rem(me + offset, count)
+        for side in range(2):
+            packed[other, part, side] = block_ref[other, part, side].T
+
+    pack(0, order[0])
+    pl.semaphore_wait(barrier, count - 1)
+
+    for part in range(groups):
+        for place, offset in enumerate(order):
+            if place + 1 < len(order):
+                pack(part, order[place + 1])
+            elif part + 1 < groups:
+                pack(part + 1, order[0])
             block_copy(part, offset).start()
-        return carry
-
-    lax.fori_loop(0, groups, start_part, 0)
-    own_copy.wait()
+
+    held[:, :, :, looks_count:] = jnp.zeros(held.shape[:3] + (held.shape[3] - looks_count,), held.dtype)
 
     def out_copy(part):
         span = pl.ds(part * group, group)
@@ -124,9 +135,19 @@
             matrix.at[:, span], coherence_ref.at[:, 0, 0, span], out_sem.at[part]
         )
 
+    def place_rows(part, side, source, rows):
+        span = pl.ds(pl.multiple_of(source * own, own), own)
+        for inner in range(group):
+            held[part * group + inner, side, span, :looks_count] = rows[inner * own : (inner + 1) * own]
+
     def compute_part(part, carry):
-        for offset in range(1, count):
+        for side in range(2):
+            place_rows(part, side, me, block_ref[me, part, side])
+        for offset in order:
             block_copy(part, offset).wait_recv()
+            source = lax.rem(me + count - offset, count)
+            for side in range(2):
+                place_rows(part, side, source, arrived[part, source, side].T)
         matrices = []
         for inner in range(group):
             window = part * group + inner
@@ -134,10 +155,10 @@
             matrix[0, window] = real
             matrix[1, window] = imag
             matrices.append(jnp.concatenate([real, imag], axis=0))
+        out_copy(part).start()
         for inner, (real, imag) in enumerate(link_windows(matrices)):
             vectors[0, pl.ds(part * group + inner, 1)] = real
             vectors[1, pl.ds(part * group + inner, 1)] = imag
-        out_copy(part).start()
         return carry
 
     lax.fori_loop(0, groups, compute_part, 0)
@@ -183,12 +204,11 @@
     dates = own_dates * count
     masked = slc * usable.astype(jnp.bfloat16)[None]
     padded_looks = pl.cdiv(looks_count, LANES) * LANES
+    group = min(per_device, max(1, LANES // own_dates))
+    groups = per_device // group
     blocks = jnp.transpose(
-        masked.reshape(2, looks_count, own_dates, count, per_device), (3, 4, 0, 2, 1)
-    )
-    blocks = jnp.pad(blocks, ((0, 0),) * 4 + ((0, padded_looks - looks_count),))
-    group = next(size for size in (4, 2, 1) if per_device % size == 0)
-    groups = per_device // group
+        masked.reshape(2, looks_count, own_dates, count * groups, group), (3, 0, 4, 2, 1)
+    ).reshape(count, groups, 2, group * own_dates, looks_count)
     return pl.pallas_call(
         functools.partial(kernel, count, looks_count, group),
         out_shape=(
@@ -201,6 +221,8 @@
             pl.BlockSpec(memory_space=pltpu.VMEM),
         ),
         scratch_shapes=[
+            pltpu.VMEM((count, groups, 2, looks_count, group * own_dates), jnp.bfloat16),
+            pltpu.VMEM((groups, count, 2, looks_count, group * own_dates), jnp.bfloat16),
             pltpu.VMEM((per_device, 2, dates, padded_looks), jnp.bfloat16),
             pltpu.VMEM((2, per_device, dates, dates), jnp.bfloat16),
             pltpu.VMEM((2, per_device, dates), jnp.float32),
@@ -208,12 +230,11 @@
             pltpu.VMEM((count, own_dates, LANES), jnp.float32),
             pltpu.SemaphoreType.DMA((groups, count)),
             pltpu.SemaphoreType.DMA((groups, count)),
-            pltpu.SemaphoreType.DMA,
             pltpu.SemaphoreType.DMA((groups,)),
             pltpu.SemaphoreType.DMA((count,)),
             pltpu.SemaphoreType.DMA((count,)),
         ],
-        compiler_params=pltpu.CompilerParams(collective_id=0, has_side_effects=True),
+        compiler_params=pltpu.CompilerParams(collective_id=0, has_side_effects=True, vmem_limit_bytes=16 << 20),
     )(blocks)
 
 

time: 46.4 us -> 38.7 us (0.83)
  Pallas kernels: 38.5 us -> 32.3 us
  local copies, waits for them, and re-layouts: 5.64 us -> 4.21 us
    pallas_call x1, Pallas kernels: 38.5 us -> 32.3 us  [local(): pl.pallas_call(functools.partial(kernel, count, looks_count, group), out_...]
    mul x1 -> x0, local copies, waits for them, and re-layouts: 1.42 us -> none  [local(): masked = slc * usable.astype(jnp.bfloat16)[None]]
    transpose x0 -> x1, local copies, waits for them, and re-layouts: none -> 1.22 us  [local(): jnp.transpose(masked.reshape(2, looks_count, own_dates, count * groups, g...]
    pad x1 -> x0, local copies, waits for them, and re-layouts: 1.2 us -> none  [local(): blocks = jnp.pad(blocks, ((0, 0),) * 4 + ((0, padded_looks - looks_count),))]
    unnamed x6 -> x5, local copies, waits for them, and re-layouts: 3.03 us -> 2.54 us
where the time goes in v2:
time: 38.7 us; the launch traced here: 38.5 us
  Pallas kernels  32.3 us (83%)
  local copies, waits for them, and re-layouts  4.21 us (11%)
  other arithmetic  1.38 us (4%)
  between operations  0.68 us (2%)
    pallas_call x1, Pallas kernels, local(): pl.pallas_call(functools.partial(kernel, count, looks_count, group), out_...  32.3 us
    unnamed x5, local copies, waits for them, and re-layouts  2.54 us
    convert_element_type x1, other arithmetic, local(): masked = slc * usable.astype(jnp.bfloat16)[None]  1.28 us
    transpose x1, local copies, waits for them, and re-layouts, local(): jnp.transpose(masked.reshape(2, looks_count, own_dates, count * groups, g...  1.22 us

profile of v2, /device:TPU:0, one launch (start us, length us, event | category | flops | bytes accessed | tf_op | source)
XLA Modules:
  0.0 38.5 jit_solution(1736806443931358890)
XLA Ops:
  0.6 0.0 copy-start
  0.6 1.3 %convert_element_type.3 = bf16[100,16,128]{2,1,0:T(8,128)(2,1)S(1)} convert(s32[100,16,128]{2,1,0:T(8,128)} %param.3) | non-fusion elementwise | flops 204800 | bytes 1228800 | tf_op jit(solution)/shard_map/convert_element_type | solution.py:205
  1.9 0.4 %copy.5 = bf16[100,16,128]{0,2,1:T(8,128)(2,1)S(1)} copy(bf16[100,16,128]{2,1,0:T(8,128)(2,1)S(1)} %convert_element_type.3) | data formatting | bytes 819200 | tf_op jit(solution)/shard_map/convert_element_type | solution.py:205
  2.4 0.0 copy-done
  2.4 1.0 %copy.6 = bf16[2,100,16,128]{1,3,2,0:T(8,128)(2,1)S(1)} copy(bf16[2,100,16,128]{3,2,1,0:T(8,128)(2,1)S(1)} %copy-done) | data formatting | bytes 1638400 | tf_op args[0]
  3.3 0.1 multiply_bitcast_fusion
  3.5 1.2 %copy.7 = bf16[16,2,8,16,100]{4,3,2,1,0:T(8,128)(2,1)S(1)} copy(bf16[16,2,8,16,100]{4,2,0,3,1:T(8,128)(2,1)S(1)} %multiply_bitcast_fusion) | data formatting | bytes 1638400 | tf_op jit(solution)/shard_map/transpose | solution.py:209
  4.7 32.3 %shard_map.41 = (bf16[2,1,1,16,128,128]{5,4,3,2,1,0:T(8,128)(2,1)S(1)}, f32[2,16,128]{2,1,0:T(8,128)S(1)}) custom-call(bf16[8,2,2,128,100]{4,3,2,1,0:T(8,128)(2,1)S(1)} %bitcast.5), custom_call_target="tpu_custom_call" | custom-call | tf_op jit(solution)/shard_map/pallas_call | solution.py:212
  37.0 1.0 %copy.10 = bf16[2,1,1,16,128,128]{5,4,3,2,1,0:T(8,128)(2,1)} copy(bf16[2,1,1,16,128,128]{5,4,3,2,1,0:T(8,128)(2,1)S(1)} %get-tuple-element.4) | data formatting | bytes 2097152
  37.9 0.6 %copy.11 = f32[2,16,128]{2,1,0:T(8,128)} copy(f32[2,16,128]{2,1,0:T(8,128)S(1)} %get-tuple-element.5) | data formatting | bytes 32768
Async XLA Ops:
  0.6 1.7 %copy-start = (bf16[2,100,16,128]{3,2,1,0:T(8,128)(2,1)S(1)}, bf16[2,100,16,128]{3,2,1,0:T(8,128)(2,1)}, u32[]{:S(2)}) copy-start(bf16[2,100,16,128]{3,2,1,0:T(8,128)(2,1)} %param.2) | copy-start | bytes 2457604

commit v3 on v2

--- a/solution.py
+++ b/solution.py
@@ -114,17 +114,17 @@
     def pack(part, offset):
         other = lax.rem(me + offset, count)
         for side in range(2):
-            packed[other, part, side] = block_ref[other, part, side].T
-
-    pack(0, order[0])
+            packed[other, part, side] = block_ref[other, part, :, side].reshape(group * own, looks_count).T
+
+    for offset in order:
+        pack(0, offset)
     pl.semaphore_wait(barrier, count - 1)
-
-    for part in range(groups):
-        for place, offset in enumerate(order):
-            if place + 1 < len(order):
-                pack(part, order[place + 1])
-            elif part + 1 < groups:
-                pack(part + 1, order[0])
+    for offset in order:
+        block_copy(0, offset).start()
+    for part in range(1, groups):
+        for offset in order:
+            pack(part, offset)
+        for offset in order:
             block_copy(part, offset).start()
 
     held[:, :, :, looks_count:] = jnp.zeros(held.shape[:3] + (held.shape[3] - looks_count,), held.dtype)
@@ -142,7 +142,7 @@
 
     def compute_part(part, carry):
         for side in range(2):
-            place_rows(part, side, me, block_ref[me, part, side])
+            place_rows(part, side, me, block_ref[me, part, :, side].reshape(group * own, looks_count))
         for offset in order:
             block_copy(part, offset).wait_recv()
             source = lax.rem(me + count - offset, count)
@@ -207,8 +207,8 @@
     group = min(per_device, max(1, LANES // own_dates))
     groups = per_device // group
     blocks = jnp.transpose(
-        masked.reshape(2, looks_count, own_dates, count * groups, group), (3, 0, 4, 2, 1)
-    ).reshape(count, groups, 2, group * own_dates, looks_count)
+        masked.reshape(2, looks_count, own_dates, count, groups, group), (3, 4, 5, 0, 2, 1)
+    )
     return pl.pallas_call(
         functools.partial(kernel, count, looks_count, group),
         out_shape=(

time: 38.7 us -> 37.5 us (0.969)
  local copies, waits for them, and re-layouts: 4.21 us -> 3.1 us
    mul x0 -> x1, local copies, waits for them, and re-layouts: none -> 1.42 us  [local(): masked = slc * usable.astype(jnp.bfloat16)[None]]
    transpose x1 -> x0, local copies, waits for them, and re-layouts: 1.22 us -> none  [local(): jnp.transpose(masked.reshape(2, looks_count, own_dates, count * groups, g...]
    unnamed x5 -> x4, local copies, waits for them, and re-layouts: 2.54 us -> 1.68 us
    convert_element_type x1 -> x0, local copies, waits for them, and re-layouts: 0.45 us -> none  [local(): masked = slc * usable.astype(jnp.bfloat16)[None]]
where the time goes in v3:
time: 37.5 us; the launch traced here: 37.3 us
  Pallas kernels  32.2 us (86%)
  local copies, waits for them, and re-layouts  3.1 us (8%)
  other arithmetic  1.36 us (4%)
  between operations  0.66 us (2%)
    pallas_call x1, Pallas kernels, local(): pl.pallas_call(functools.partial(kernel, count, looks_count, group), out_...  32.2 us
    unnamed x4, local copies, waits for them, and re-layouts  1.68 us
    mul x1, local copies, waits for them, and re-layouts, local(): masked = slc * usable.astype(jnp.bfloat16)[None]  1.42 us
    convert_element_type x1, other arithmetic, local(): masked = slc * usable.astype(jnp.bfloat16)[None]  1.28 us

profile of v3, /device:TPU:0, one launch (start us, length us, event | category | flops | bytes accessed | tf_op | source)
XLA Modules:
  0.0 37.3 jit_solution(13548286504779491765)
XLA Ops:
  0.6 0.0 copy-start
  0.6 1.3 %convert_element_type.3 = bf16[100,16,128]{2,1,0:T(8,128)(2,1)S(1)} convert(s32[100,16,128]{2,1,0:T(8,128)} %param.3) | non-fusion elementwise | flops 204800 | bytes 1228800 | tf_op jit(solution)/shard_map/convert_element_type | solution.py:205
  1.9 0.1 copy-done
  2.0 0.1 broadcast_multiply_fusion
  2.1 1.4 %copy.4 = bf16[2,100,16,128]{1,2,0,3:T(8,128)(2,1)S(1)} copy(bf16[2,100,16,128]{3,2,1,0:T(8,128)(2,1)S(1)} %broadcast_multiply_fusion) | data formatting | bytes 1638400 | tf_op jit(solution)/shard_map/mul | solution.py:205
  3.5 32.2 %shard_map.41 = (bf16[2,1,1,16,128,128]{5,4,3,2,1,0:T(8,128)(2,1)S(1)}, f32[2,16,128]{2,1,0:T(8,128)S(1)}) custom-call(bf16[8,2,8,2,16,100]{5,4,3,2,1,0:T(8,128)(2,1)S(1)} %bitcast.3), custom_call_target="tpu_custom_call" | custom-call | tf_op jit(solution)/shard_map/pallas_call | solution.py:212
  35.7 1.0 %copy.7 = bf16[2,1,1,16,128,128]{5,4,3,2,1,0:T(8,128)(2,1)} copy(bf16[2,1,1,16,128,128]{5,4,3,2,1,0:T(8,128)(2,1)S(1)} %get-tuple-element.4) | data formatting | bytes 2097152
  36.7 0.6 %copy.8 = f32[2,16,128]{2,1,0:T(8,128)} copy(f32[2,16,128]{2,1,0:T(8,128)S(1)} %get-tuple-element.5) | data formatting | bytes 32768
Async XLA Ops:
  0.6 1.4 %copy-start = (bf16[2,100,16,128]{3,2,1,0:T(8,128)(2,1)S(1)}, bf16[2,100,16,128]{3,2,1,0:T(8,128)(2,1)}, u32[]{:S(2)}) copy-start(bf16[2,100,16,128]{3,2,1,0:T(8,128)(2,1)} %param.2) | copy-start | bytes 2457604

commit v4 on v3

--- a/solution.py
+++ b/solution.py
@@ -75,7 +75,7 @@
 
 def send_order(count):
     middle = count // 2
-    return sorted(range(1, count), key=lambda offset: abs(offset - middle))
+    return sorted(range(1, count), key=lambda offset: (abs(offset - middle) > middle // 2, offset % 2 == 0, offset))
 
 
 def kernel(
@@ -97,7 +97,6 @@
             device_id_type=pl.DeviceIdType.MESH,
         )
 
-    mine = pl.ds(pl.multiple_of(me * own, own), own)
     order = send_order(count)
 
     def block_copy(part, offset):
@@ -113,8 +112,9 @@
 
     def pack(part, offset):
         other = lax.rem(me + offset, count)
-        for side in range(2):
-            packed[other, part, side] = block_ref[other, part, :, side].reshape(group * own, looks_count).T
+        packed[other, part] = jnp.concatenate(
+            [block_ref[other, part, :, side].reshape(group * own, looks_count).T for side in range(2)], axis=0
+        )
 
     for offset in order:
         pack(0, offset)
@@ -146,8 +146,9 @@
         for offset in order:
             block_copy(part, offset).wait_recv()
             source = lax.rem(me + count - offset, count)
+            rows = arrived[part, source].T
             for side in range(2):
-                place_rows(part, side, source, arrived[part, source, side].T)
+                place_rows(part, side, source, rows[:, side * looks_count : (side + 1) * looks_count])
         matrices = []
         for inner in range(group):
             window = part * group + inner
@@ -163,12 +164,20 @@
 
     lax.fori_loop(0, groups, compute_part, 0)
 
-    turned[:, : 2 * windows] = jnp.concatenate([vectors[0], vectors[1]], axis=0).T
+    fold, rows, width = own // turned.shape[1], turned.shape[1], 2 * windows
+    spread = jnp.concatenate([vectors[0], vectors[1]], axis=0)
+    spread = jnp.pad(spread, ((0, LANES - width), (0, 0))).T.reshape(count, fold, rows, LANES)
+    folded = spread[:, 0]
+    for place in range(1, fold):
+        folded = folded + pltpu.roll(
+            spread[:, place].reshape(count * rows, LANES), place * width, 1
+        ).reshape(count, rows, LANES)
+    turned[...] = folded
 
     def back_copy(offset):
         other = lax.rem(me + offset, count)
         return pltpu.make_async_remote_copy(
-            src_ref=turned.at[pl.ds(pl.multiple_of(other * own, own), own)],
+            src_ref=turned.at[other],
             dst_ref=landed.at[me],
             send_sem=back_send.at[offset],
             recv_sem=back_recv.at[offset],
@@ -178,13 +187,15 @@
 
     for offset in range(1, count):
         back_copy(offset).start()
-    landed[me] = turned[mine]
+    landed[me] = turned[me]
     for offset in range(1, count):
         back_copy(offset).wait_recv()
     for side in range(2):
-        linked_ref[side] = jnp.concatenate(
-            [landed[source][:, side * windows : (side + 1) * windows] for source in range(count)], axis=1
-        )
+        for place in range(fold):
+            first = place * width + side * windows
+            linked_ref[side, place * rows : (place + 1) * rows] = jnp.concatenate(
+                [landed[source][:, first : first + windows] for source in range(count)], axis=1
+            )
 
     def finish_part(part, carry):
         for offset in range(1, count):
@@ -206,6 +217,8 @@
     padded_looks = pl.cdiv(looks_count, LANES) * LANES
     group = min(per_device, max(1, LANES // own_dates))
     groups = per_device // group
+    fold = max(1, own_dates // 8)
+    fold = fold if own_dates % fold == 0 and 2 * per_device * fold <= LANES else 1
     blocks = jnp.transpose(
         masked.reshape(2, looks_count, own_dates, count, groups, group), (3, 4, 5, 0, 2, 1)
     )
@@ -221,13 +234,13 @@
             pl.BlockSpec(memory_space=pltpu.VMEM),
         ),
         scratch_shapes=[
-            pltpu.VMEM((count, groups, 2, looks_count, group * own_dates), jnp.bfloat16),
-            pltpu.VMEM((groups, count, 2, looks_count, group * own_dates), jnp.bfloat16),
+            pltpu.VMEM((count, groups, 2 * looks_count, group * own_dates), jnp.bfloat16),
+            pltpu.VMEM((groups, count, 2 * looks_count, group * own_dates), jnp.bfloat16),
             pltpu.VMEM((per_device, 2, dates, padded_looks), jnp.bfloat16),
             pltpu.VMEM((2, per_device, dates, dates), jnp.bfloat16),
             pltpu.VMEM((2, per_device, dates), jnp.float32),
-            pltpu.VMEM((dates, LANES), jnp.float32),
-            pltpu.VMEM((count, own_dates, LANES), jnp.float32),
+            pltpu.VMEM((count, own_dates // fold, LANES), jnp.float32),
+            pltpu.VMEM((count, own_dates // fold, LANES), jnp.float32),
             pltpu.SemaphoreType.DMA((groups, count)),
             pltpu.SemaphoreType.DMA((groups, count)),
             pltpu.SemaphoreType.DMA((groups,)),

time: 37.5 us -> 36.8 us (0.981)
  Pallas kernels: 32.2 us -> 31.5 us
    pallas_call x1, Pallas kernels: 32.2 us -> 31.5 us  [local(): pl.pallas_call(functools.partial(kernel, count, looks_count, group), out_...]
where the time goes in v4:
time: 36.8 us; the launch traced here: 36.7 us
  Pallas kernels  31.5 us (86%)
  local copies, waits for them, and re-layouts  3.1 us (8%)
  other arithmetic  1.36 us (4%)
  between operations  0.66 us (2%)
    pallas_call x1, Pallas kernels, local(): pl.pallas_call(functools.partial(kernel, count, looks_count, group), out_...  31.5 us
    unnamed x4, local copies, waits for them, and re-layouts  1.68 us
    mul x1, local copies, waits for them, and re-layouts, local(): masked = slc * usable.astype(jnp.bfloat16)[None]  1.42 us
    convert_element_type x1, other arithmetic, local(): masked = slc * usable.astype(jnp.bfloat16)[None]  1.28 us

profile of v4, /device:TPU:0, one launch (start us, length us, event | category | flops | bytes accessed | tf_op | source)
XLA Modules:
  0.0 36.7 jit_solution(1682604664481046575)
XLA Ops:
  0.6 0.0 copy-start
  0.6 1.3 %convert_element_type.3 = bf16[100,16,128]{2,1,0:T(8,128)(2,1)S(1)} convert(s32[100,16,128]{2,1,0:T(8,128)} %param.3) | non-fusion elementwise | flops 204800 | bytes 1228800 | tf_op jit(solution)/shard_map/convert_element_type | solution.py:216
  1.9 0.1 copy-done
  2.0 0.1 broadcast_multiply_fusion
  2.1 1.4 %copy.4 = bf16[2,100,16,128]{1,2,0,3:T(8,128)(2,1)S(1)} copy(bf16[2,100,16,128]{3,2,1,0:T(8,128)(2,1)S(1)} %broadcast_multiply_fusion) | data formatting | bytes 1638400 | tf_op jit(solution)/shard_map/mul | solution.py:216
  3.5 31.5 %shard_map.41 = (bf16[2,1,1,16,128,128]{5,4,3,2,1,0:T(8,128)(2,1)S(1)}, f32[2,16,128]{2,1,0:T(8,128)S(1)}) custom-call(bf16[8,2,8,2,16,100]{5,4,3,2,1,0:T(8,128)(2,1)S(1)} %bitcast.3), custom_call_target="tpu_custom_call" | custom-call | tf_op jit(solution)/shard_map/pallas_call | solution.py:225
  35.1 1.0 %copy.7 = bf16[2,1,1,16,128,128]{5,4,3,2,1,0:T(8,128)(2,1)} copy(bf16[2,1,1,16,128,128]{5,4,3,2,1,0:T(8,128)(2,1)S(1)} %get-tuple-element.4) | data formatting | bytes 2097152
  36.1 0.6 %copy.8 = f32[2,16,128]{2,1,0:T(8,128)} copy(f32[2,16,128]{2,1,0:T(8,128)S(1)} %get-tuple-element.5) | data formatting | bytes 32768
Async XLA Ops:
  0.6 1.4 %copy-start = (bf16[2,100,16,128]{3,2,1,0:T(8,128)(2,1)S(1)}, bf16[2,100,16,128]{3,2,1,0:T(8,128)(2,1)}, u32[]{:S(2)}) copy-start(bf16[2,100,16,128]{3,2,1,0:T(8,128)(2,1)} %param.2) | copy-start | bytes 2457604

commit v5 on v4

--- a/solution.py
+++ b/solution.py
@@ -9,6 +9,7 @@
 
 ITERS = 4
 LANES = 128
+PIECES = 2
 NT = (((1,), (1,)), ((), ()))
 
 
@@ -81,8 +82,8 @@
 def kernel(
     count, looks_count, group,
     block_ref, coherence_ref, linked_ref,
-    packed, arrived, held, matrix, vectors, turned, landed,
-    send_sem, recv_sem, out_sem, back_send, back_recv,
+    packed, arrived, held, vectors, turned, landed,
+    send_sem, recv_sem, back_send, back_recv,
 ):
     me = lax.axis_index("date")
     windows = held.shape[0]
@@ -128,12 +129,6 @@
             block_copy(part, offset).start()
 
     held[:, :, :, looks_count:] = jnp.zeros(held.shape[:3] + (held.shape[3] - looks_count,), held.dtype)
-
-    def out_copy(part):
-        span = pl.ds(part * group, group)
-        return pltpu.make_async_copy(
-            matrix.at[:, span], coherence_ref.at[:, 0, 0, span], out_sem.at[part]
-        )
 
     def place_rows(part, side, source, rows):
         span = pl.ds(pl.multiple_of(source * own, own), own)
@@ -153,10 +148,9 @@
         for inner in range(group):
             window = part * group + inner
             real, imag = window_coherence(held[window, 0], held[window, 1], looks_count)
-            matrix[0, window] = real
-            matrix[1, window] = imag
+            coherence_ref[0, 0, 0, window] = real
+            coherence_ref[1, 0, 0, window] = imag
             matrices.append(jnp.concatenate([real, imag], axis=0))
-        out_copy(part).start()
         for inner, (real, imag) in enumerate(link_windows(matrices)):
             vectors[0, pl.ds(part * group + inner, 1)] = real
             vectors[1, pl.ds(part * group + inner, 1)] = imag
@@ -200,12 +194,32 @@
     def finish_part(part, carry):
         for offset in range(1, count):
             block_copy(part, offset).wait_send()
-        out_copy(part).wait()
         return carry
 
     lax.fori_loop(0, groups, finish_part, 0)
     for offset in range(1, count):
         back_copy(offset).wait_send()
+
+
+def deliver(coherence_in, linked_in, coherence_out, linked_out, sem):
+    copies = [pltpu.make_async_copy(linked_in, linked_out, sem.at[0])]
+    windows = coherence_in.shape[3]
+    pieces = PIECES if windows % PIECES == 0 else 1
+    size = windows // pieces
+    for side in range(coherence_in.shape[0]):
+        for piece in range(pieces):
+            span = pl.ds(piece * size, size)
+            copies.append(
+                pltpu.make_async_copy(
+                    coherence_in.at[side, :, :, span],
+                    coherence_out.at[side, :, :, span],
+                    sem.at[1 + side * PIECES + piece],
+                )
+            )
+    for copy in copies:
+        copy.start()
+    for copy in copies:
+        copy.wait()
 
 
 def local(slc, usable):
@@ -222,7 +236,7 @@
     blocks = jnp.transpose(
         masked.reshape(2, looks_count, own_dates, count, groups, group), (3, 4, 5, 0, 2, 1)
     )
-    return pl.pallas_call(
+    results = pl.pallas_call(
         functools.partial(kernel, count, looks_count, group),
         out_shape=(
             jax.ShapeDtypeStruct((2, 1, 1, per_device, dates, dates), jnp.bfloat16),
@@ -230,25 +244,31 @@
         ),
         in_specs=[pl.BlockSpec(memory_space=pltpu.VMEM)],
         out_specs=(
-            pl.BlockSpec(memory_space=pl.ANY),
+            pl.BlockSpec(memory_space=pltpu.VMEM),
             pl.BlockSpec(memory_space=pltpu.VMEM),
         ),
         scratch_shapes=[
             pltpu.VMEM((count, groups, 2 * looks_count, group * own_dates), jnp.bfloat16),
             pltpu.VMEM((groups, count, 2 * looks_count, group * own_dates), jnp.bfloat16),
             pltpu.VMEM((per_device, 2, dates, padded_looks), jnp.bfloat16),
-            pltpu.VMEM((2, per_device, dates, dates), jnp.bfloat16),
             pltpu.VMEM((2, per_device, dates), jnp.float32),
             pltpu.VMEM((count, own_dates // fold, LANES), jnp.float32),
             pltpu.VMEM((count, own_dates // fold, LANES), jnp.float32),
             pltpu.SemaphoreType.DMA((groups, count)),
             pltpu.SemaphoreType.DMA((groups, count)),
-            pltpu.SemaphoreType.DMA((groups,)),
             pltpu.SemaphoreType.DMA((count,)),
             pltpu.SemaphoreType.DMA((count,)),
         ],
         compiler_params=pltpu.CompilerParams(collective_id=0, has_side_effects=True, vmem_limit_bytes=16 << 20),
     )(blocks)
+    return pl.pallas_call(
+        deliver,
+        out_shape=tuple(jax.ShapeDtypeStruct(array.shape, array.dtype) for array in results),
+        in_specs=[pl.BlockSpec(memory_space=pl.ANY)] * 2,
+        out_specs=(pl.BlockSpec(memory_space=pl.ANY),) * 2,
+        scratch_shapes=[pltpu.SemaphoreType.DMA((results[0].shape[0] * PIECES + 1,))],
+        compiler_params=pltpu.CompilerParams(vmem_limit_bytes=1 << 20),
+    )(*results)
 
 
 def solution(mesh):

time: 36.8 us -> 36.1 us (0.981)
  local copies, waits for them, and re-layouts: 3.1 us -> 1.52 us
  Pallas kernels: 31.5 us -> 32.4 us
    unnamed x4 -> x2, local copies, waits for them, and re-layouts: 1.68 us -> 0.11 us
    pallas_call x0 -> x1, Pallas kernels: none -> 1.01 us  [local(): pl.pallas_call(deliver, out_shape=tuple((jax.ShapeDtypeStruct(array.shape...]
where the time goes in v5:
time: 36.1 us; the launch traced here: 35.9 us
  Pallas kernels  32.4 us (90%)
  local copies, waits for them, and re-layouts  1.52 us (4%)
  other arithmetic  1.36 us (4%)
  between operations  0.66 us (2%)
    pallas_call x1, Pallas kernels, local(): pl.pallas_call(functools.partial(kernel, count, looks_count, group), out_...  31.4 us
    mul x1, local copies, waits for them, and re-layouts, local(): masked = slc * usable.astype(jnp.bfloat16)[None]  1.42 us
    convert_element_type x1, other arithmetic, local(): masked = slc * usable.astype(jnp.bfloat16)[None]  1.28 us
    pallas_call x1, Pallas kernels, local(): pl.pallas_call(deliver, out_shape=tuple((jax.ShapeDtypeStruct(array.shape...  1.01 us

profile of v5, /device:TPU:0, one launch (start us, length us, event | category | flops | bytes accessed | tf_op | source)
XLA Modules:
  0.0 35.9 jit_solution(3446243290807739139)
XLA Ops:
  0.6 0.0 copy-start
  0.6 1.3 %convert_element_type.3 = bf16[100,16,128]{2,1,0:T(8,128)(2,1)S(1)} convert(s32[100,16,128]{2,1,0:T(8,128)} %param.3) | non-fusion elementwise | flops 204800 | bytes 1228800 | tf_op jit(solution)/shard_map/convert_element_type | solution.py:230
  1.9 0.1 copy-done
  2.0 0.1 broadcast_multiply_fusion
  2.1 1.4 %copy.4 = bf16[2,100,16,128]{1,2,0,3:T(8,128)(2,1)S(1)} copy(bf16[2,100,16,128]{3,2,1,0:T(8,128)(2,1)S(1)} %broadcast_multiply_fusion) | data formatting | bytes 1638400 | tf_op jit(solution)/shard_map/mul | solution.py:230
  3.5 31.4 %shard_map.41 = (bf16[2,1,1,16,128,128]{5,4,3,2,1,0:T(8,128)(2,1)S(1)}, f32[2,16,128]{2,1,0:T(8,128)S(1)}) custom-call(bf16[8,2,8,2,16,100]{5,4,3,2,1,0:T(8,128)(2,1)S(1)} %bitcast.3), custom_call_target="tpu_custom_call" | custom-call | tf_op jit(solution)/shard_map/pallas_call | solution.py:239
  34.9 1.0 %shard_map.42 = (bf16[2,1,1,16,128,128]{5,4,3,2,1,0:T(8,128)(2,1)}, f32[2,16,128]{2,1,0:T(8,128)}) custom-call(bf16[2,1,1,16,128,128]{5,4,3,2,1,0:T(8,128)(2,1)S(1)} %get-tuple-element.4.coherence_in, f32[2,16,128]{2,1,0:T(8,128)S(1)} %get-tuple-element.5.linked_in), custom_call_target="tpu_custom_call" | custom-call | tf_op jit(solution)/shard_map/pallas_call | solution.py:264
Async XLA Ops:
  0.6 1.4 %copy-start = (bf16[2,100,16,128]{3,2,1,0:T(8,128)(2,1)S(1)}, bf16[2,100,16,128]{3,2,1,0:T(8,128)(2,1)}, u32[]{:S(2)}) copy-start(bf16[2,100,16,128]{3,2,1,0:T(8,128)(2,1)} %param.2) | copy-start | bytes 2457604

commit v6 on v5

--- a/solution.py
+++ b/solution.py
@@ -76,7 +76,7 @@
 
 def send_order(count):
     middle = count // 2
-    return sorted(range(1, count), key=lambda offset: (abs(offset - middle) > middle // 2, offset % 2 == 0, offset))
+    return sorted(range(1, count), key=lambda offset: (offset % 2 == 0, -abs(offset - middle), offset))
 
 
 def kernel(

time: 36.1 us -> 35.6 us (0.986)
  Pallas kernels: 32.4 us -> 31.9 us
    pallas_call x1, Pallas kernels: 31.4 us -> 30.9 us  [local(): pl.pallas_call(functools.partial(kernel, count, looks_count, group), out_...]
where the time goes in v6:
time: 35.6 us; the launch traced here: 35.5 us
  Pallas kernels  31.9 us (90%)
  local copies, waits for them, and re-layouts  1.52 us (4%)
  other arithmetic  1.36 us (4%)
  between operations  0.66 us (2%)
    pallas_call x1, Pallas kernels, local(): pl.pallas_call(functools.partial(kernel, count, looks_count, group), out_...  30.9 us
    mul x1, local copies, waits for them, and re-layouts, local(): masked = slc * usable.astype(jnp.bfloat16)[None]  1.42 us
    convert_element_type x1, other arithmetic, local(): masked = slc * usable.astype(jnp.bfloat16)[None]  1.28 us
    pallas_call x1, Pallas kernels, local(): pl.pallas_call(deliver, out_shape=tuple((jax.ShapeDtypeStruct(array.shape...  1.01 us

profile of v6, /device:TPU:0, one launch (start us, length us, event | category | flops | bytes accessed | tf_op | source)
XLA Modules:
  0.0 35.5 jit_solution(17702490499008922616)
XLA Ops:
  0.6 0.0 copy-start
  0.6 1.3 %convert_element_type.3 = bf16[100,16,128]{2,1,0:T(8,128)(2,1)S(1)} convert(s32[100,16,128]{2,1,0:T(8,128)} %param.3) | non-fusion elementwise | flops 204800 | bytes 1228800 | tf_op jit(solution)/shard_map/convert_element_type | solution.py:230
  1.9 0.1 copy-done
  2.0 0.1 broadcast_multiply_fusion
  2.1 1.4 %copy.4 = bf16[2,100,16,128]{1,2,0,3:T(8,128)(2,1)S(1)} copy(bf16[2,100,16,128]{3,2,1,0:T(8,128)(2,1)S(1)} %broadcast_multiply_fusion) | data formatting | bytes 1638400 | tf_op jit(solution)/shard_map/mul | solution.py:230
  3.5 30.9 %shard_map.41 = (bf16[2,1,1,16,128,128]{5,4,3,2,1,0:T(8,128)(2,1)S(1)}, f32[2,16,128]{2,1,0:T(8,128)S(1)}) custom-call(bf16[8,2,8,2,16,100]{5,4,3,2,1,0:T(8,128)(2,1)S(1)} %bitcast.3), custom_call_target="tpu_custom_call" | custom-call | tf_op jit(solution)/shard_map/pallas_call | solution.py:239
  34.5 1.0 %shard_map.42 = (bf16[2,1,1,16,128,128]{5,4,3,2,1,0:T(8,128)(2,1)}, f32[2,16,128]{2,1,0:T(8,128)}) custom-call(bf16[2,1,1,16,128,128]{5,4,3,2,1,0:T(8,128)(2,1)S(1)} %get-tuple-element.4.coherence_in, f32[2,16,128]{2,1,0:T(8,128)S(1)} %get-tuple-element.5.linked_in), custom_call_target="tpu_custom_call" | custom-call | tf_op jit(solution)/shard_map/pallas_call | solution.py:264
Async XLA Ops:
  0.6 1.4 %copy-start = (bf16[2,100,16,128]{3,2,1,0:T(8,128)(2,1)S(1)}, bf16[2,100,16,128]{3,2,1,0:T(8,128)(2,1)}, u32[]{:S(2)}) copy-start(bf16[2,100,16,128]{3,2,1,0:T(8,128)(2,1)} %param.2) | copy-start | bytes 2457604
